TPU v7x, 32 devices: a whole 2x2x4 slice. The times are simulated.
32 devices in a mesh: dp: 16 (over z, y, x), head: 2 (over core).
Axes of the slice: x: 2, y: 2, z: 4, core: 2. Of those that a mesh axis runs over, the one named last changes fastest.
Arguments:
- hidden: bfloat16 [64, 512, 3584], P(('dp', 'head')), may hold values from -6 to 6
- head_proj: bfloat16 [4, 3584, 128], P('head'), may hold values from -0.09375 to 0.09375
- head_out: bfloat16 [4, 128], P('head'), may hold values from -0.8984375 to 0.8984375
- head_ratio: int32 [4], replicated, may hold values from 2 to 7
- group_of: int32 [64], replicated, may hold values from 0 to 3, as said below
- lengths: int32 [64], P(('dp', 'head')), may hold values from 1 to 512
- token_mask: int32 [64, 512], P(('dp', 'head')), may hold values 0 or 1
Outputs:
- advantages: float32 [64, 512], P(('dp', 'head'))
Inputs may be any that keep to these rules, and one draw needn't show every extreme that they name: `group_of`: every one of the 4 groups holds exactly 16 rollouts.
All inputs are finite; a program needn't handle non-finite values. No bound on the sum of `token_mask` on one device may be relied on, other than what follows from the above.
Results may differ from a plain program's by a relative error of at most 0.0026.
Values may be sent and summed in bfloat16 or wider, within the bound.
A program may use at most 64 MiB of HBM per device.

v0:
```python
import functools

import jax
import jax.numpy as jnp
from jax import lax
from jax.experimental import pallas as pl
from jax.experimental.pallas import tpu as pltpu
from jax.sharding import PartitionSpec as P

GROUP = 16
MESH = pl.DeviceIdType.MESH

token_weight = 0.5
gap_weight = 0.5
clip_limit = 2.0
var_offset = 0.04

DEPTH_PIECES = 2
PACK = 16


def kernel(
    chips,
    hidden, proj, readout, ratio, groups, lens, mask, out,
    rows_all, w_own, w_other, out_own, out_other, acc, comb, ends, msg, slots,
    ratio_s, groups_s, lens_s, groups_v, mask_v,
    row_sem, w_sem, small_sem, pair_send, pair_recv, all_send, all_recv,
):
    chip, core = lax.axis_index("dp"), lax.axis_index("head")
    width = hidden.shape[2]
    count, seq = mask.shape
    heads, _, rank = proj.shape
    devices = 2 * chips
    me = 2 * chip + core
    total_rows = count * seq
    depth = width // DEPTH_PIECES
    lanes = msg.shape[1]

    loads = [pltpu.make_async_copy(lens, lens_s, small_sem.at[0])]
    loads.append(pltpu.make_async_copy(ratio, ratio_s, small_sem.at[1]))
    loads.append(pltpu.make_async_copy(groups, groups_s, small_sem.at[2]))
    loads.append(pltpu.make_async_copy(readout, out_own, small_sem.at[3]))
    loads.append(pltpu.make_async_copy(groups, groups_v.at[0], small_sem.at[4]))
    loads.append(pltpu.make_async_copy(mask, mask_v, small_sem.at[5]))
    w_loads = [
        pltpu.make_async_copy(proj.at[k], w_own.at[:, pl.ds(k * rank, rank)], w_sem.at[k])
        for k in range(heads)
    ]
    cuts = [pl.ds(d * depth, depth) for d in range(DEPTH_PIECES)]
    h_loads = [
        pltpu.make_async_copy(hidden.at[:, :, cuts[d]], rows_all.at[:, :, cuts[d]], row_sem.at[d])
        for d in range(DEPTH_PIECES)
    ]
    for copy in loads[:1] + h_loads + w_loads + loads[1:]:
        copy.start()

    barrier = pltpu.get_barrier_semaphore()

    def each_other(act):
        def both(step, _):
            there = lax.rem(chip + step, chips)
            act((there, core))
            act((there, 1 - core))
            return 0

        if chips <= 16:
            for step in range(1, chips):
                both(step, 0)
        else:
            lax.fori_loop(1, chips, both, 0)
        act((chip, 1 - core))

    each_other(
        lambda place: pl.semaphore_signal(barrier, inc=1, device_id=place, device_id_type=MESH)
    )

    for copy in loads[:1] + h_loads:
        copy.wait()

    sub = lax.broadcasted_iota(jnp.int32, (PACK, width), 0)
    picked = jnp.zeros((PACK, width), jnp.float32)
    for r in range(count):
        last = lens_s[r] - 1
        block = rows_all[r * (seq // PACK) + lax.div(last, PACK)].astype(jnp.float32)
        row = jnp.sum(jnp.where(sub == lax.rem(last, PACK), block, 0.0), axis=0, keepdims=True)
        picked = jnp.where(sub == r, jnp.broadcast_to(row, (PACK, width)), picked)
    ends[pl.ds(0, PACK), :] = picked.astype(jnp.bfloat16)

    pl.semaphore_wait(barrier, devices - 1)

    def to_pair(src, dst, k):
        return pltpu.make_async_remote_copy(
            src_ref=src, dst_ref=dst, send_sem=pair_send.at[k], recv_sem=pair_recv.at[k],
            device_id=(chip, 1 - core), device_id_type=MESH,
        )

    send_ends = to_pair(ends.at[pl.ds(0, PACK)], ends.at[pl.ds(PACK, PACK)], 0)
    send_out = to_pair(out_own, out_other, 1)
    send_w = [
        to_pair(w_own.at[cuts[d]], w_other.at[cuts[d]], 2 + d)
        for d in range(DEPTH_PIECES)
    ]
    send_ends.start()
    for copy in w_loads + loads[1:]:
        copy.wait()
    send_out.start()
    send_w[0].start()

    weights = [ratio_s[k].astype(jnp.float32) for k in range(2 * heads)]
    weight_sum = sum(weights[1:], weights[0])
    own_mix = [
        ratio_s[core * heads + k].astype(jnp.float32) / weight_sum for k in range(heads)
    ]
    other_mix = [
        ratio_s[(1 - core) * heads + k].astype(jnp.float32) / weight_sum for k in range(heads)
    ]

    def reader(values):
        wide = values[...].astype(jnp.float32)
        line = lax.broadcasted_iota(jnp.int32, (8, rank), 0)
        parts = [
            jnp.where(line == k, jnp.broadcast_to(wide[k : k + 1], (8, rank)), 0.0)
            for k in range(heads)
        ]
        return jnp.concatenate(parts, axis=1).astype(jnp.bfloat16)

    def scores(inner, lhs, mix):
        active = jnp.tanh(inner).astype(jnp.bfloat16)
        per_head = lax.dot_general(
            lhs, active, (((1,), (1,)), ((), ())), preferred_element_type=jnp.float32
        )
        line = mix[0] * per_head[0:1]
        for k in range(1, heads):
            line = line + mix[k] * per_head[k : k + 1]
        return line

    own_lhs = reader(out_own)

    def partial(values, d):
        rows = rows_all[:, :, cuts[d]].reshape(total_rows, depth)
        return jnp.dot(rows, values[cuts[d], :], preferred_element_type=jnp.float32)

    def add_partial(values, d):
        inner = partial(values, d)
        if d > 0:
            inner = acc[...] + inner
        if d < DEPTH_PIECES - 1:
            acc[...] = inner
        return inner

    add_partial(w_own, 0)
    send_ends.wait_recv()

    inner = jnp.dot(ends[...], w_own[...], preferred_element_type=jnp.float32)
    active = jnp.tanh(inner).astype(jnp.bfloat16).astype(jnp.float32)
    wide = out_own[...].astype(jnp.float32)
    scale = jnp.concatenate([own_mix[k] * wide[k : k + 1] for k in range(heads)], axis=1)
    part = jnp.sum(active * scale, axis=1, keepdims=True)
    line = lax.broadcasted_iota(jnp.int32, (2 * PACK, lanes), 0)
    lane = lax.broadcasted_iota(jnp.int32, (2 * PACK, lanes), 1)
    mine = (line < count) & (lane == me * count + line)
    theirs = (line >= PACK) & (line < PACK + count) & (
        lane == (4 * chip + 1 - me) * count + line - PACK
    )
    note = jnp.sum(jnp.where(mine | theirs, part, 0.0), axis=0, keepdims=True)
    msg[...] = note
    slots[me] = note

    each_other(
        lambda place: pltpu.make_async_remote_copy(
            src_ref=msg, dst_ref=slots.at[me], send_sem=all_send, recv_sem=all_recv,
            device_id=place, device_id_type=MESH,
        ).start()
    )
    for copy in send_w[1:]:
        copy.start()

    for d in range(1, DEPTH_PIECES):
        inner = add_partial(w_own, d)
    comb[...] = scores(inner, own_lhs, own_mix)

    send_out.wait_recv()
    other_lhs = reader(out_other)
    for d in range(DEPTH_PIECES):
        send_w[d].wait_recv()
        inner = add_partial(w_other, d)
    comb[...] = comb[...] + scores(inner, other_lhs, other_mix)

    rest = slots.at[pl.ds(0, devices - 1)]
    pltpu.make_async_copy(rest, rest, all_recv).wait()

    reward = jnp.sum(slots[...], axis=0)[:, : groups_v.shape[1]]
    labels = groups_v[...]
    shape = (count, reward.shape[1])
    rollout = lax.broadcasted_iota(jnp.int32, shape, 0)
    lane_of = lax.broadcasted_iota(jnp.int32, shape, 1)
    wide = jnp.broadcast_to(reward, shape)
    group = jnp.zeros(shape, jnp.int32)
    length = jnp.zeros((count, seq), jnp.int32)
    line = lax.broadcasted_iota(jnp.int32, (count, seq), 0)
    for r in range(count):
        group = jnp.where(rollout == r, groups_s[me * count + r], group)
        length = jnp.where(line == r, lens_s[r], length)
    member = jnp.broadcast_to(labels, shape) == group
    own = jnp.sum(jnp.where(lane_of == me * count + rollout, wide, 0.0), axis=1, keepdims=True)
    mean = jnp.sum(jnp.where(member, wide, 0.0), axis=1, keepdims=True) / GROUP
    gap = wide - mean
    var = jnp.sum(jnp.where(member, gap * gap, 0.0), axis=1, keepdims=True) / GROUP
    best = jnp.max(jnp.where(member, wide, -jnp.inf), axis=1, keepdims=True)
    base = (own - mean) / jnp.sqrt(var + var_offset) - gap_weight * (best - own)
    shaped = base + token_weight * jnp.concatenate(
        [comb[:, pl.ds(r * seq, seq)] for r in range(count)], axis=0
    )
    place = lax.broadcasted_iota(jnp.int32, (count, seq), 1)
    valid = (place < length) & (mask_v[...] == 1)
    out[...] = jnp.where(valid, jnp.clip(shaped, -clip_limit, clip_limit), 0.0)

    send_ends.wait_send()
    send_out.wait_send()
    for copy in send_w:
        copy.wait_send()
    pltpu.make_async_copy(rest, rest, all_send).wait()


def solution(mesh):
    chips = mesh.shape["dp"]

    def on_device(hidden, head_proj, head_out, head_ratio, group_of, lengths, token_mask):
        count, seq, width = hidden.shape
        heads, _, rank = head_proj.shape
        everyone = group_of.shape[0]
        lanes = -(-everyone // 128) * 128
        hbm = pl.BlockSpec(memory_space=pltpu.HBM)
        bf16, f32, i32 = jnp.bfloat16, jnp.float32, jnp.int32
        return pl.pallas_call(
            functools.partial(kernel, chips),
            out_shape=jax.ShapeDtypeStruct((count, seq), f32),
            in_specs=[hbm] * 7,
            out_specs=pl.BlockSpec(memory_space=pltpu.VMEM),
            scratch_shapes=[
                pltpu.VMEM((count * seq // PACK, PACK, width), bf16),
                pltpu.VMEM((width, heads * rank), bf16),
                pltpu.VMEM((width, heads * rank), bf16),
                pltpu.VMEM((heads, rank), bf16),
                pltpu.VMEM((heads, rank), bf16),
                pltpu.VMEM((count * seq, heads * rank), f32),
                pltpu.VMEM((1, count * seq), f32),
                pltpu.VMEM((2 * PACK, width), bf16),
                pltpu.VMEM((1, lanes), f32),
                pltpu.VMEM((2 * chips, 1, lanes), f32),
                pltpu.SMEM(head_ratio.shape, i32),
                pltpu.SMEM(group_of.shape, i32),
                pltpu.SMEM(lengths.shape, i32),
                pltpu.VMEM((1, everyone), i32),
                pltpu.VMEM((count, seq), i32),
                pltpu.SemaphoreType.DMA((DEPTH_PIECES,)),
                pltpu.SemaphoreType.DMA((heads,)),
                pltpu.SemaphoreType.DMA((6,)),
                pltpu.SemaphoreType.DMA((2 + DEPTH_PIECES,)),
                pltpu.SemaphoreType.DMA((2 + DEPTH_PIECES,)),
                pltpu.SemaphoreType.DMA,
                pltpu.SemaphoreType.DMA,
            ],
            compiler_params=pltpu.CompilerParams(
                collective_id=0, has_side_effects=True, vmem_limit_bytes=60 * 1024 * 1024
            ),
            name="advantages",
        )(hidden.reshape(-1, PACK, width), head_proj, head_out, head_ratio, group_of, lengths, token_mask)

    return jax.shard_map(
        on_device,
        mesh=mesh,
        in_specs=(
            P(("dp", "head"), None, None),
            P("head", None, None),
            P("head", None),
            P(),
            P(),
            P(("dp", "head")),
            P(("dp", "head"), None),
        ),
        out_specs=P(("dp", "head"), None),
        check_vma=False,
    )
```

profile of v0, /device:TPU:0, one launch (start us, length us, event | category | flops | bytes accessed | tf_op | source)
XLA Modules:
  0.0 17.9 jit_solution(9065194966350801919)
XLA Ops:
  0.0 16.6 %advantages.1 = f32[2,512]{1,0:T(2,128)} custom-call(bf16[64,16,3584]{2,1,0:T(8,128)(2,1)} %bitcast.1, bf16[2,3584,128]{2,1,0:T(8,128)(2,1)} %proj.1, bf16[2,128]{1,0:T(2,128)(2,1)} %readout.1, s32[4]{0:T(128)} %ratio.1, s32[64]{0:T(128)} %groups.1, s32[2]{0:T(128)} %lens.1, s32[2,512]{1,0:T(2,128)} %mask.1), custom_call_target="tpu_custom_call" | custom-call | tf_op jit(solution)/shard_map/advantages/pallas_call | solution.py:235
  16.6 1.3 %copy.9 = f32[2,512]{1,0:T(2,128)} copy(f32[2,512]{1,0:T(2,128)} %advantages.1) | data formatting | bytes 8192
where the time goes:
time: 18.1 us; the launch traced here: 17.9 us
  Pallas kernels  16.6 us (92%)
  local copies, waits for them, and re-layouts  1.28 us (7%)
    pallas_call x1, Pallas kernels, on_device(): pl.pallas_call(functools.partial(kernel, chips), out_shape=jax.ShapeDtype...  16.6 us
    unnamed x1, local copies, waits for them, and re-layouts  1.28 us

commit v1 on v0

--- a/solution.py
+++ b/solution.py
@@ -234,7 +234,7 @@
         bf16, f32, i32 = jnp.bfloat16, jnp.float32, jnp.int32
         return pl.pallas_call(
             functools.partial(kernel, chips),
-            out_shape=jax.ShapeDtypeStruct((count, seq), f32),
+            out_shape=pltpu.VMEM((count, seq), f32),
             in_specs=[hbm] * 7,
             out_specs=pl.BlockSpec(memory_space=pltpu.VMEM),
             scratch_shapes=[

time: 18.1 us -> 16.8 us (0.928)
  local copies, waits for them, and re-layouts: 1.28 us -> 0.6 us
  Pallas kernels: 16.6 us -> 16 us
    unnamed x1, local copies, waits for them, and re-layouts: 1.28 us -> 0.6 us
    pallas_call x1, Pallas kernels: 16.6 us -> 16 us  [on_device(): pl.pallas_call(functools.partial(kernel, chips), out_shape=pltpu.VMEM((co...]
where the time goes in v1:
time: 16.8 us; the launch traced here: 16.6 us
  Pallas kernels  16 us (95%)
  local copies, waits for them, and re-layouts  0.6 us (4%)
    pallas_call x1, Pallas kernels, on_device(): pl.pallas_call(functools.partial(kernel, chips), out_shape=pltpu.VMEM((co...  16 us
    unnamed x1, local copies, waits for them, and re-layouts  0.6 us

profile of v1, /device:TPU:0, one launch (start us, length us, event | category | flops | bytes accessed | tf_op | source)
XLA Modules:
  0.0 16.6 jit_solution(4486392198426040604)
XLA Ops:
  0.0 16.0 %advantages.1 = f32[2,512]{1,0:T(2,128)S(1)} custom-call(bf16[64,16,3584]{2,1,0:T(8,128)(2,1)} %bitcast.1, bf16[2,3584,128]{2,1,0:T(8,128)(2,1)} %proj.1, bf16[2,128]{1,0:T(2,128)(2,1)} %readout.1, s32[4]{0:T(128)} %ratio.1, s32[64]{0:T(128)} %groups.1, s32[2]{0:T(128)} %lens.1, s32[2,512]{1,0:T(2,128)} %mask.1), custom_call_target="tpu_custom_call" | custom-call | tf_op jit(solution)/shard_map/advantages/pallas_call | solution.py:235
  16.0 0.6 %copy.9 = f32[2,512]{1,0:T(2,128)} copy(f32[2,512]{1,0:T(2,128)S(1)} %advantages.1) | data formatting | bytes 8192

commit v2 on v1

v2 whole, which is shorter than its diff:
```python
import functools

import jax
import jax.numpy as jnp
from jax import lax
from jax.experimental import pallas as pl
from jax.experimental.pallas import tpu as pltpu
from jax.sharding import PartitionSpec as P

GROUP = 16
MESH = pl.DeviceIdType.MESH

token_weight = 0.5
gap_weight = 0.5
clip_limit = 2.0
var_offset = 0.04

PACK = 16
LINES = 8
TILE = 256
UNITS = 2
CUT = 6
STEP = 3
AHEAD = 8


def kernel(
    chips,
    hidden, proj, readout, ratio, groups, lens, mask, out,
    rows_all, w_own, w_other, out_own, out_other, comb, ends, msg, slots,
    ratio_s, groups_s, lens_s, groups_v, mask_v,
    pair_recv, all_recv,
):
    chip, core = lax.axis_index("dp"), lax.axis_index("head")
    width = hidden.shape[2]
    count, seq = mask.shape
    heads, _, rank = proj.shape
    devices = 2 * chips
    me = 2 * chip + core
    total_rows = count * seq
    lanes = msg.shape[1]
    tiles = width // TILE
    share = tiles // UNITS
    blocks = total_rows // UNITS // TILE
    pieces = [range(at, min(at + STEP, tiles)) for at in range(0, tiles, STEP)]
    ahead = chip < max(1, chips // AHEAD)

    def columns(span):
        return pl.ds(span[0] * TILE, len(span) * TILE)

    def each_other(act):
        def both(step, _):
            there = lax.rem(chip + step, chips)
            act((there, core))
            act((there, 1 - core))
            return 0

        if chips <= 16:
            for step in range(1, chips):
                both(step, 0)
        else:
            lax.fori_loop(1, chips, both, 0)
        act((chip, 1 - core))

    def reader(values):
        wide = values[...].astype(jnp.float32)
        line = lax.broadcasted_iota(jnp.int32, (PACK, rank), 0)
        parts = [
            jnp.where(line == k, jnp.broadcast_to(wide[k : k + 1], (PACK, rank)), 0.0)
            for k in range(heads)
        ]
        return jnp.concatenate(parts, axis=1).astype(jnp.bfloat16)

    def body(sums, lines, brief, row_sem, w_sem, small_sem, pair_send, all_send):
        first = pltpu.make_async_copy(lens, lens_s, small_sem.at[0])
        small = [
            pltpu.make_async_copy(ratio, ratio_s, small_sem.at[1]),
            pltpu.make_async_copy(groups, groups_s, small_sem.at[2]),
            pltpu.make_async_copy(readout, out_own, small_sem.at[3]),
            pltpu.make_async_copy(groups, groups_v.at[0], small_sem.at[4]),
            pltpu.make_async_copy(mask, mask_v, small_sem.at[5]),
        ]
        w_loads = [
            pltpu.make_async_copy(proj.at[k], w_own.at[:, pl.ds(k * rank, rank)], w_sem.at[k])
            for k in range(heads)
        ]
        h_loads = [
            pltpu.make_async_copy(
                hidden.at[:, :, columns(span)], rows_all.at[:, :, columns(span)], row_sem.at[d]
            )
            for d, span in enumerate([range(CUT), range(CUT, tiles)])
        ]
        for copy in [first] + h_loads:
            copy.start()

        barrier = pltpu.get_barrier_semaphore()
        each_other(
            lambda place: pl.semaphore_signal(
                barrier, inc=1, device_id=place, device_id_type=MESH
            )
        )

        def to_pair(src, dst, k):
            return pltpu.make_async_remote_copy(
                src_ref=src, dst_ref=dst, send_sem=pair_send.at[k], recv_sem=pair_recv.at[k],
                device_id=(chip, 1 - core), device_id_type=MESH,
            )

        send_ends = to_pair(ends.at[0], ends.at[1], 0)
        send_out = to_pair(out_own, out_other, 1)
        send_w = [
            to_pair(w_own.at[columns(span)], w_other.at[columns(span)], 2 + d)
            for d, span in enumerate(pieces)
        ]

        for unit in range(UNITS):
            for ref in sums[unit] + lines[unit] + brief[unit : unit + 1]:
                pltpu.matmul_pop(ref)

        def rows(unit, block, k):
            start = (unit * blocks + block) * (TILE // PACK)
            part = rows_all[pl.ds(start, TILE // PACK), :, pl.ds(k * TILE, TILE)]
            return part.reshape(TILE, TILE)

        def add_tiles(values, span):
            for k in span:
                for unit in range(UNITS):
                    pltpu.matmul_push_rhs(values[pl.ds(k * TILE, TILE), :], k % 2, unit)
                    for block in range(blocks):
                        pltpu.matmul_acc_lhs(
                            sums[unit][block], rows(unit, block, k), None if block else k % 2
                        )

        def add_scores(values, mix, fresh):
            lhs = reader(values)
            for block in range(blocks):
                for unit in range(UNITS):
                    inner = pltpu.matmul_pop(sums[unit][block])
                    active = jnp.tanh(inner).astype(jnp.bfloat16)
                    pltpu.matmul_push_rhs(active, block % 2, unit, transpose=True)
                    pltpu.matmul_acc_lhs(lines[unit][block], lhs, block % 2)
            for block in range(blocks):
                for unit in range(UNITS):
                    per_head = pltpu.matmul_pop(lines[unit][block])
                    line = mix[0] * per_head[0:1]
                    for k in range(1, heads):
                        line = line + mix[k] * per_head[k : k + 1]
                    at = pl.ds((unit * blocks + block) * TILE, TILE)
                    comb[:, at] = line if fresh else comb[:, at] + line

        with jax.named_scope("wait_mid"):
            h_loads[0].wait()
        for copy in w_loads + small:
            copy.start()
        with jax.named_scope("wait_rest"):
            h_loads[1].wait()
            first.wait()

        sub = lax.broadcasted_iota(jnp.int32, (PACK, width), 0)
        picked = jnp.zeros((PACK, width), jnp.float32)
        for r in range(count):
            last = lens_s[r] - 1
            block = rows_all[r * (seq // PACK) + lax.div(last, PACK)].astype(jnp.float32)
            row = jnp.sum(jnp.where(sub == lax.rem(last, PACK), block, 0.0), axis=0, keepdims=True)
            picked = jnp.where(sub == r, jnp.broadcast_to(row, (PACK, width)), picked)
        ends[0] = picked.astype(jnp.bfloat16)[:LINES]

        def mixture(part):
            weights = [ratio_s[k].astype(jnp.float32) for k in range(2 * heads)]
            weight_sum = sum(weights[1:], weights[0])
            return [
                ratio_s[part * heads + k].astype(jnp.float32) / weight_sum for k in range(heads)
            ]

        def own_heads():
            with jax.named_scope("own_tiles"):
                add_tiles(w_own, range(tiles))
            with jax.named_scope("own_scores"):
                add_scores(out_own, mixture(core), True)

        @pl.when(ahead)
        def _():
            for copy in w_loads + small:
                copy.wait()
            own_heads()

        with jax.named_scope("wait_barrier"):
            pl.semaphore_wait(barrier, devices - 1)
        send_ends.start()


        @pl.when(jnp.logical_not(ahead))
        def _():
            with jax.named_scope("wait_w"):
                for copy in w_loads + small:
                    copy.wait()

        send_out.start()

        @pl.when(ahead)
        def _():
            for copy in send_w:
                copy.start()

        own_mix = mixture(core)

        def stage(k):
            for unit in range(UNITS):
                pltpu.matmul_push_rhs(
                    w_own[pl.ds((unit * share + k) * TILE, TILE), :], k % 2, unit
                )

        with jax.named_scope("stage"):
            for k in range(2):
                stage(k)
        with jax.named_scope("wait_ends"):
            send_ends.wait_recv()
        with jax.named_scope("ends_dot"):
            both = ends[...].reshape(2 * LINES, width)
            for k in range(share):
                for unit in range(UNITS):
                    at = (unit * share + k) * TILE
                    pltpu.matmul_acc_lhs(brief[unit], both[:, at : at + TILE], k % 2)
                if k + 2 < share:
                    stage(k + 2)
            inner = pltpu.matmul_pop(brief[0]) + pltpu.matmul_pop(brief[1])
            active = jnp.tanh(inner).astype(jnp.bfloat16).astype(jnp.float32)
            wide = out_own[...].astype(jnp.float32)
            scale = jnp.concatenate([own_mix[k] * wide[k : k + 1] for k in range(heads)], axis=1)
            part = jnp.sum(active * scale, axis=1, keepdims=True)
            line = lax.broadcasted_iota(jnp.int32, (2 * LINES, lanes), 0)
            lane = lax.broadcasted_iota(jnp.int32, (2 * LINES, lanes), 1)
            mine = (line < count) & (lane == me * count + line)
            theirs = (line >= LINES) & (line < LINES + count) & (
                lane == (4 * chip + 1 - me) * count + line - LINES
            )
            note = jnp.sum(jnp.where(mine | theirs, part, 0.0), axis=0, keepdims=True)
            msg[...] = note
            slots[me] = note

        with jax.named_scope("send_all"):
            each_other(
                lambda place: pltpu.make_async_remote_copy(
                    src_ref=msg, dst_ref=slots.at[me], send_sem=all_send.at[0],
                    recv_sem=all_recv, device_id=place, device_id_type=MESH,
                ).start()
            )

        @pl.when(jnp.logical_not(ahead))
        def _():
            for copy in send_w:
                copy.start()
            own_heads()

        send_out.wait_recv()
        for d, span in enumerate(pieces):
            with jax.named_scope(f"wait_other{d}"):
                send_w[d].wait_recv()
            with jax.named_scope(f"other{d}"):
                add_tiles(w_other, span)
        with jax.named_scope("other_scores"):
            add_scores(out_other, mixture(1 - core), False)

        send_ends.wait_send()
        send_out.wait_send()
        for copy in send_w:
            copy.wait_send()
        rest = slots.at[pl.ds(0, devices - 1)]
        pltpu.make_async_copy(rest, rest, all_send.at[0]).wait()

    def acc(unit, size):
        return pltpu.ACC(unit)((size, TILE), jnp.float32)

    pl.run_scoped(
        body,
        [[acc(unit, TILE) for _ in range(blocks)] for unit in range(UNITS)],
        [[acc(unit, PACK) for _ in range(blocks)] for unit in range(UNITS)],
        [acc(unit, 2 * LINES) for unit in range(UNITS)],
        pltpu.SemaphoreType.DMA((2,)),
        pltpu.SemaphoreType.DMA((heads,)),
        pltpu.SemaphoreType.DMA((6,)),
        pltpu.SemaphoreType.DMA((2 + len(pieces),)),
        pltpu.SemaphoreType.DMA((1,)),
    )

    labels = groups_v[...]
    shape = (count, labels.shape[1])
    rollout = lax.broadcasted_iota(jnp.int32, shape, 0)
    lane_of = lax.broadcasted_iota(jnp.int32, shape, 1)
    group = jnp.zeros(shape, jnp.int32)
    length = jnp.zeros((count, seq), jnp.int32)
    line = lax.broadcasted_iota(jnp.int32, (count, seq), 0)
    for r in range(count):
        group = jnp.where(rollout == r, groups_s[me * count + r], group)
        length = jnp.where(line == r, lens_s[r], length)
    member = jnp.broadcast_to(labels, shape) == group
    place = lax.broadcasted_iota(jnp.int32, (count, seq), 1)
    valid = (place < length) & (mask_v[...] == 1)
    tokens = token_weight * jnp.concatenate(
        [comb[:, pl.ds(r * seq, seq)] for r in range(count)], axis=0
    )

    rest = slots.at[pl.ds(0, devices - 1)]
    with jax.named_scope("wait_all"):
        pltpu.make_async_copy(rest, rest, all_recv).wait()

    with jax.named_scope("final"):
        reward = jnp.sum(slots[...], axis=0)[:, : labels.shape[1]]
        wide = jnp.broadcast_to(reward, shape)
        own = jnp.sum(
            jnp.where(lane_of == me * count + rollout, wide, 0.0), axis=1, keepdims=True
        )
        mean = jnp.sum(jnp.where(member, wide, 0.0), axis=1, keepdims=True) / GROUP
        gap = wide - mean
        var = jnp.sum(jnp.where(member, gap * gap, 0.0), axis=1, keepdims=True) / GROUP
        best = jnp.max(jnp.where(member, wide, -jnp.inf), axis=1, keepdims=True)
        base = (own - mean) / jnp.sqrt(var + var_offset) - gap_weight * (best - own)
        shaped = base + tokens
        out[...] = jnp.where(valid, jnp.clip(shaped, -clip_limit, clip_limit), 0.0)


def solution(mesh):
    chips = mesh.shape["dp"]

    def on_device(hidden, head_proj, head_out, head_ratio, group_of, lengths, token_mask):
        count, seq, width = hidden.shape
        heads, _, rank = head_proj.shape
        everyone = group_of.shape[0]
        lanes = -(-everyone // 128) * 128
        pieces = -(-width // (STEP * TILE))
        hbm = pl.BlockSpec(memory_space=pltpu.HBM)
        bf16, f32, i32 = jnp.bfloat16, jnp.float32, jnp.int32
        return pl.pallas_call(
            functools.partial(kernel, chips),
            out_shape=pltpu.VMEM((count, seq), f32),
            in_specs=[hbm] * 7,
            out_specs=pl.BlockSpec(memory_space=pltpu.VMEM),
            scratch_shapes=[
                pltpu.VMEM((count * seq // PACK, PACK, width), bf16),
                pltpu.VMEM((width, heads * rank), bf16),
                pltpu.VMEM((width, heads * rank), bf16),
                pltpu.VMEM((heads, rank), bf16),
                pltpu.VMEM((heads, rank), bf16),
                pltpu.VMEM((1, count * seq), f32),
                pltpu.VMEM((2, LINES, width), bf16),
                pltpu.VMEM((1, lanes), f32),
                pltpu.VMEM((2 * chips, 1, lanes), f32),
                pltpu.SMEM(head_ratio.shape, i32),
                pltpu.SMEM(group_of.shape, i32),
                pltpu.SMEM(lengths.shape, i32),
                pltpu.VMEM((1, everyone), i32),
                pltpu.VMEM((count, seq), i32),
                pltpu.SemaphoreType.DMA((2 + pieces,)),
                pltpu.SemaphoreType.DMA,
            ],
            compiler_params=pltpu.CompilerParams(
                collective_id=0, has_side_effects=True, vmem_limit_bytes=60 * 1024 * 1024
            ),
            name="advantages",
        )(hidden.reshape(-1, PACK, width), head_proj, head_out, head_ratio, group_of, lengths, token_mask)

    return jax.shard_map(
        on_device,
        mesh=mesh,
        in_specs=(
            P(("dp", "head"), None, None),
            P("head", None, None),
            P("head", None),
            P(),
            P(),
            P(("dp", "head")),
            P(("dp", "head"), None),
        ),
        out_specs=P(("dp", "head"), None),
        check_vma=False,
    )
```

time: 16.8 us -> 13.9 us (0.83)
  Pallas kernels: 16 us -> 13.1 us
    pallas_call x1, Pallas kernels: 16 us -> 13.1 us  [on_device(): pl.pallas_call(functools.partial(kernel, chips), out_shape=pltpu.VMEM((co...]
where the time goes in v2:
time: 13.9 us; the launch traced here: 13.7 us
  Pallas kernels  13.1 us (94%)
  local copies, waits for them, and re-layouts  0.6 us (4%)
    pallas_call x1, Pallas kernels, on_device(): pl.pallas_call(functools.partial(kernel, chips), out_shape=pltpu.VMEM((co...  13.1 us
    unnamed x1, local copies, waits for them, and re-layouts  0.6 us

profile of v2, /device:TPU:0, one launch (start us, length us, event | category | flops | bytes accessed | tf_op | source)
XLA Modules:
  0.0 13.7 jit_solution(4639830107611451892)
XLA Ops:
  0.0 13.1 %advantages.1 = f32[2,512]{1,0:T(2,128)S(1)} custom-call(bf16[64,16,3584]{2,1,0:T(8,128)(2,1)} %bitcast.1, bf16[2,3584,128]{2,1,0:T(8,128)(2,1)} %proj.1, bf16[2,128]{1,0:T(2,128)(2,1)} %readout.1, s32[4]{0:T(128)} %ratio.1, s32[64]{0:T(128)} %groups.1, s32[2]{0:T(128)} %lens.1, s32[2,512]{1,0:T(2,128)} %mask.1), custom_call_target="tpu_custom_call" | custom-call | tf_op jit(solution)/shard_map/advantages/pallas_call | solution.py:333
  13.1 0.6 %copy.9 = f32[2,512]{1,0:T(2,128)} copy(f32[2,512]{1,0:T(2,128)S(1)} %advantages.1) | data formatting | bytes 8192

commit v3 on v2

v3 whole, which is shorter than its diff:
```python
import functools

import jax
import jax.numpy as jnp
from jax import lax
from jax.experimental import pallas as pl
from jax.experimental.pallas import tpu as pltpu
from jax.sharding import PartitionSpec as P

GROUP = 16
MESH = pl.DeviceIdType.MESH

token_weight = 0.5
gap_weight = 0.5
clip_limit = 2.0
var_offset = 0.04

PACK = 16
LINES = 8
TILE = 256
UNITS = 2
FAN = 32
AHEAD = 4
FRONT = 8


def mixture(ratio_s, part, heads):
    weights = [ratio_s[k].astype(jnp.float32) for k in range(2 * heads)]
    weight_sum = sum(weights[1:], weights[0])
    return [ratio_s[part * heads + k].astype(jnp.float32) / weight_sum for k in range(heads)]


def gather(
    hidden, proj, readout, ratio, lens, w_front, ends_own, out_own, scale,
    found, lens_s, ratio_s,
):
    core = lax.axis_index("head")
    count = found.shape[0]
    heads, width, rank = proj.shape
    blocks = hidden.shape[0] // count

    def body(sem, w_sem, row_sem):
        first = pltpu.make_async_copy(lens, lens_s, sem.at[0])
        small = [
            pltpu.make_async_copy(ratio, ratio_s, sem.at[1]),
            pltpu.make_async_copy(readout, out_own, sem.at[2]),
        ]
        w_loads = [
            pltpu.make_async_copy(
                proj.at[k, pl.ds(0, FRONT * TILE)], w_front.at[:, pl.ds(k * rank, rank)],
                w_sem.at[k],
            )
            for k in range(heads)
        ]
        for copy in [first] + small + w_loads:
            copy.start()
        with jax.named_scope("gather_lens"):
            first.wait()
        last = [lens_s[r] - 1 for r in range(count)]
        row_loads = [
            pltpu.make_async_copy(
                hidden.at[r * blocks + lax.div(last[r], LINES)], found.at[r], row_sem.at[r]
            )
            for r in range(count)
        ]
        for copy in row_loads:
            copy.start()
        for copy in small:
            copy.wait()
        mix = mixture(ratio_s, core, heads)
        wide = out_own[...].astype(jnp.float32)
        scale[...] = jnp.concatenate([mix[k] * wide[k : k + 1] for k in range(heads)], axis=1)
        with jax.named_scope("gather_rows"):
            for copy in row_loads:
                copy.wait()
        sub = lax.broadcasted_iota(jnp.int32, (LINES, width), 0)
        picked = jnp.zeros((LINES, width), jnp.float32)
        for r in range(count):
            at = sub == lax.rem(last[r], LINES)
            row = jnp.sum(
                jnp.where(at, found[r].astype(jnp.float32), 0.0), axis=0, keepdims=True
            )
            picked = jnp.where(sub == r, jnp.broadcast_to(row, (LINES, width)), picked)
        ends_own[...] = picked.astype(jnp.bfloat16)
        with jax.named_scope("gather_w"):
            for copy in w_loads:
                copy.wait()

    pl.run_scoped(
        body,
        pltpu.SemaphoreType.DMA((3,)),
        pltpu.SemaphoreType.DMA((heads,)),
        pltpu.SemaphoreType.DMA((count,)),
    )


def kernel(
    chips,
    hidden, proj, w_front, ends_own, out_own, scale, ratio, groups, lens, mask, out,
    rows_all, w_back, w_other, out_other, comb, ends, msg, slots,
    ratio_s, groups_s, lens_s, groups_v, mask_v,
    pair_recv, all_recv, here,
):
    chip, core = lax.axis_index("dp"), lax.axis_index("head")
    width = hidden.shape[2]
    count, seq = mask.shape
    heads, rank = out_own.shape
    devices = 2 * chips
    me = 2 * chip + core
    total_rows = count * seq
    lanes = msg.shape[1]
    tiles = width // TILE
    spans = [range(FRONT), range(FRONT, tiles)]
    blocks = total_rows // UNITS // TILE
    pieces = [range(FRONT), range(FRONT, tiles)]
    ahead = chip < max(1, chips // AHEAD)

    def columns(span):
        return pl.ds(span[0] * TILE, len(span) * TILE)

    def cores(act, low, high):
        def both(there, _):
            act((there, core))
            act((there, 1 - core))
            return 0

        lax.fori_loop(low, high, both, 0)

    def reader(values):
        wide = values[...].astype(jnp.float32)
        line = lax.broadcasted_iota(jnp.int32, (PACK, rank), 0)
        parts = [
            jnp.where(line == k, jnp.broadcast_to(wide[k : k + 1], (PACK, rank)), 0.0)
            for k in range(heads)
        ]
        return jnp.concatenate(parts, axis=1).astype(jnp.bfloat16)

    def body(sums, lines, brief, row_sem, w_sem, small_sem, pair_send, all_send):
        small = [
            pltpu.make_async_copy(ratio, ratio_s, small_sem.at[0]),
            pltpu.make_async_copy(lens, lens_s, small_sem.at[1]),
            pltpu.make_async_copy(groups, groups_s, small_sem.at[2]),
            pltpu.make_async_copy(groups, groups_v.at[0], small_sem.at[3]),
            pltpu.make_async_copy(mask, mask_v, small_sem.at[4]),
        ]
        h_loads = [
            pltpu.make_async_copy(
                hidden.at[:, :, columns(span)], rows_all.at[:, :, columns(span)], row_sem.at[d]
            )
            for d, span in enumerate(spans)
        ]
        w_loads = [
            pltpu.make_async_copy(
                proj.at[k, columns(range(FRONT, tiles))], w_back.at[:, pl.ds(k * rank, rank)],
                w_sem.at[k],
            )
            for k in range(heads)
        ]
        for copy in w_loads:
            copy.start()

        barrier = pltpu.get_barrier_semaphore()

        def hello(place):
            pl.semaphore_signal(barrier, inc=1, device_id=place, device_id_type=MESH)

        hello((chip, 1 - core))
        for copy in h_loads + small:
            copy.start()
        cores(hello, chip + 1, chips)
        ends[0] = ends_own[...]

        def to_pair(src, dst, k):
            return pltpu.make_async_remote_copy(
                src_ref=src, dst_ref=dst, send_sem=pair_send.at[k], recv_sem=pair_recv.at[k],
                device_id=(chip, 1 - core), device_id_type=MESH,
            )

        send_ends = to_pair(ends_own, ends.at[1], 0)
        send_out = to_pair(out_own, out_other, 1)
        def own_piece(span):
            return w_front if span[0] < FRONT else w_back

        send_w = [
            to_pair(own_piece(span), w_other.at[columns(span)], 2 + d)
            for d, span in enumerate(pieces)
        ]

        for unit in range(UNITS):
            for ref in sums[unit] + lines[unit] + brief[unit : unit + 1]:
                pltpu.matmul_pop(ref)

        def own_tile(k):
            ref, at = (w_front, k) if k < FRONT else (w_back, k - FRONT)
            return ref[pl.ds(at * TILE, TILE), :]

        def other_tile(k):
            return w_other[pl.ds(k * TILE, TILE), :]

        def rows(unit, block, k):
            start = (unit * blocks + block) * (TILE // PACK)
            part = rows_all[pl.ds(start, TILE // PACK), :, pl.ds(k * TILE, TILE)]
            return part.reshape(TILE, TILE)

        def add_tiles(tile, span):
            for k in span:
                for unit in range(UNITS):
                    pltpu.matmul_push_rhs(tile(k), k % 2, unit)
                    for block in range(blocks):
                        pltpu.matmul_acc_lhs(
                            sums[unit][block], rows(unit, block, k), None if block else k % 2
                        )

        def add_scores(values, mix, fresh):
            lhs = reader(values)
            for block in range(blocks):
                for unit in range(UNITS):
                    inner = pltpu.matmul_pop(sums[unit][block])
                    active = jnp.tanh(inner).astype(jnp.bfloat16)
                    pltpu.matmul_push_rhs(active, block % 2, unit, transpose=True)
                    pltpu.matmul_acc_lhs(lines[unit][block], lhs, block % 2)
            for block in range(blocks):
                for unit in range(UNITS):
                    per_head = pltpu.matmul_pop(lines[unit][block])
                    line = mix[0] * per_head[0:1]
                    for k in range(1, heads):
                        line = line + mix[k] * per_head[k : k + 1]
                    at = pl.ds((unit * blocks + block) * TILE, TILE)
                    comb[:, at] = line if fresh else comb[:, at] + line

        def own_heads():
            for d, span in enumerate(spans):
                with jax.named_scope(f"wait_hidden{d}"):
                    h_loads[d].wait()
                with jax.named_scope(f"own_tiles{d}"):
                    add_tiles(own_tile, span)
            with jax.named_scope("own_scores"):
                small[0].wait()
                add_scores(out_own, mixture(ratio_s, core, heads), True)

        with jax.named_scope("wait_barrier"):
            pl.semaphore_wait(barrier, 2 * chip + 1)
        send_ends.start()
        send_out.start()

        @pl.when(ahead)
        def _():
            send_w[0].start()

        cores(
            lambda place: pl.semaphore_signal(
                here, inc=1, device_id=place, device_id_type=MESH
            ),
            0, chip,
        )

        turns = [range(at, at + UNITS) for at in range(0, tiles, UNITS)]

        def stage(turn):
            for unit, k in enumerate(turns[turn]):
                pltpu.matmul_push_rhs(own_tile(k), turn % 2, unit)

        for turn in range(2):
            stage(turn)
        with jax.named_scope("wait_w"):
            for copy in w_loads:
                copy.wait()

        @pl.when(ahead)
        def _():
            send_w[1].start()

        with jax.named_scope("wait_ends"):
            send_ends.wait_recv()
        with jax.named_scope("ends_dot"):
            both = ends[...].reshape(2 * LINES, width)
            for turn, units in enumerate(turns):
                for unit, k in enumerate(units):
                    at = k * TILE
                    pltpu.matmul_acc_lhs(brief[unit], both[:, at : at + TILE], turn % 2)
                if turn + 2 < len(turns):
                    stage(turn + 2)
            inner = pltpu.matmul_pop(brief[0]) + pltpu.matmul_pop(brief[1])
            active = jnp.tanh(inner).astype(jnp.bfloat16).astype(jnp.float32)
            part = jnp.sum(active * scale[...], axis=1, keepdims=True)
            line = lax.broadcasted_iota(jnp.int32, (2 * LINES, lanes), 0)
            lane = lax.broadcasted_iota(jnp.int32, (2 * LINES, lanes), 1)
            mine = (line < count) & (lane == me * count + line)
            theirs = (line >= LINES) & (line < LINES + count) & (
                lane == (4 * chip + 1 - me) * count + line - LINES
            )
            found = jnp.where(mine | theirs, part, 0.0)
            found = found[:LINES] + found[LINES:]
            note = sum([found[r : r + 1] for r in range(1, count)], found[:1])
            msg[...] = note
            slots[me] = note

        def tell(place):
            pltpu.make_async_remote_copy(
                src_ref=msg, dst_ref=slots.at[me], send_sem=all_send.at[0],
                recv_sem=all_recv, device_id=place, device_id_type=MESH,
            ).start()

        with jax.named_scope("send_lower"):
            cores(tell, 0, chip)
            tell((chip, 1 - core))

        @pl.when(ahead)
        def _():
            own_heads()

        @pl.when(chip < chips - 1)
        def _():
            with jax.named_scope("wait_higher"):
                pl.semaphore_wait(here, devices - 2 - 2 * chip)

        with jax.named_scope("send_higher"):
            cores(tell, chip + 1, chips)

        @pl.when(jnp.logical_not(ahead))
        def _():
            for copy in send_w:
                copy.start()
            own_heads()

        send_out.wait_recv()
        for d, span in enumerate(pieces):
            with jax.named_scope(f"wait_other{d}"):
                send_w[d].wait_recv()
            with jax.named_scope(f"other{d}"):
                add_tiles(other_tile, span)
        with jax.named_scope("other_scores"):
            add_scores(out_other, mixture(ratio_s, 1 - core, heads), False)

        for copy in small[1:]:
            copy.wait()
        send_ends.wait_send()
        send_out.wait_send()
        for copy in send_w:
            copy.wait_send()
        rest = slots.at[pl.ds(0, devices - 1)]
        pltpu.make_async_copy(rest, rest, all_send.at[0]).wait()

    def acc(unit, size):
        return pltpu.ACC(unit)((size, TILE), jnp.float32)

    pl.run_scoped(
        body,
        [[acc(unit, TILE) for _ in range(blocks)] for unit in range(UNITS)],
        [[acc(unit, PACK) for _ in range(blocks)] for unit in range(UNITS)],
        [acc(unit, 2 * LINES) for unit in range(UNITS)],
        pltpu.SemaphoreType.DMA((2,)),
        pltpu.SemaphoreType.DMA((heads,)),
        pltpu.SemaphoreType.DMA((5,)),
        pltpu.SemaphoreType.DMA((2 + len(pieces),)),
        pltpu.SemaphoreType.DMA((1,)),
    )

    labels = groups_v[...]
    shape = (count, labels.shape[1])
    rollout = lax.broadcasted_iota(jnp.int32, shape, 0)
    lane_of = lax.broadcasted_iota(jnp.int32, shape, 1)
    group = jnp.zeros(shape, jnp.int32)
    length = jnp.zeros((count, seq), jnp.int32)
    line = lax.broadcasted_iota(jnp.int32, (count, seq), 0)
    for r in range(count):
        group = jnp.where(rollout == r, groups_s[me * count + r], group)
        length = jnp.where(line == r, lens_s[r], length)
    member = jnp.broadcast_to(labels, shape) == group
    place = lax.broadcasted_iota(jnp.int32, (count, seq), 1)
    valid = (place < length) & (mask_v[...] == 1)
    tokens = token_weight * jnp.concatenate(
        [comb[:, pl.ds(r * seq, seq)] for r in range(count)], axis=0
    )

    rest = slots.at[pl.ds(0, devices - 1)]
    with jax.named_scope("wait_all"):
        pltpu.make_async_copy(rest, rest, all_recv).wait()

    with jax.named_scope("final"):
        level = [slots[k] for k in range(min(devices, FAN))]
        for k in range(FAN, devices):
            level[k % FAN] = level[k % FAN] + slots[k]
        while len(level) > 1:
            level = [sum(level[k + 1 : k + 2], level[k]) for k in range(0, len(level), 2)]
        reward = level[0][:, : labels.shape[1]]
        wide = jnp.broadcast_to(reward, shape)
        own = jnp.sum(
            jnp.where(lane_of == me * count + rollout, wide, 0.0), axis=1, keepdims=True
        )
        mean = jnp.sum(jnp.where(member, wide, 0.0), axis=1, keepdims=True) * (1 / GROUP)
        gap = wide - mean
        var = jnp.sum(jnp.where(member, gap * gap, 0.0), axis=1, keepdims=True) * (1 / GROUP)
        best = jnp.max(jnp.where(member, wide, -jnp.inf), axis=1, keepdims=True)
        base = (own - mean) * lax.rsqrt(var + var_offset) - gap_weight * (best - own)
        shaped = base + tokens
        out[...] = jnp.where(valid, jnp.clip(shaped, -clip_limit, clip_limit), 0.0)


def solution(mesh):
    chips = mesh.shape["dp"]

    def on_device(hidden, head_proj, head_out, head_ratio, group_of, lengths, token_mask):
        count, seq, width = hidden.shape
        heads, _, rank = head_proj.shape
        everyone = group_of.shape[0]
        lanes = -(-everyone // 128) * 128
        pieces = 2
        hbm = pl.BlockSpec(memory_space=pltpu.HBM)
        bf16, f32, i32 = jnp.bfloat16, jnp.float32, jnp.int32
        vmem = pl.BlockSpec(memory_space=pltpu.VMEM)
        rows = hidden.reshape(-1, PACK, width)
        early = pl.pallas_call(
            gather,
            out_shape=[
                pltpu.VMEM((FRONT * TILE, heads * rank), bf16),
                pltpu.VMEM((LINES, width), bf16),
                pltpu.VMEM((heads, rank), bf16),
                pltpu.VMEM((1, heads * rank), f32),
            ],
            in_specs=[hbm] * 5,
            out_specs=[vmem] * 4,
            scratch_shapes=[
                pltpu.VMEM((count, LINES, width), bf16),
                pltpu.SMEM(lengths.shape, i32),
                pltpu.SMEM(head_ratio.shape, i32),
            ],
            compiler_params=pltpu.CompilerParams(vmem_limit_bytes=60 * 1024 * 1024),
            name="gather",
        )(hidden.reshape(-1, LINES, width), head_proj, head_out, head_ratio, lengths)
        early = [pltpu.with_memory_space_constraint(value, pltpu.VMEM) for value in early]
        return pl.pallas_call(
            functools.partial(kernel, chips),
            out_shape=pltpu.VMEM((count, seq), f32),
            in_specs=[hbm] * 2 + [vmem] * 4 + [hbm] * 4,
            out_specs=pl.BlockSpec(memory_space=pltpu.VMEM),
            scratch_shapes=[
                pltpu.VMEM((count * seq // PACK, PACK, width), bf16),
                pltpu.VMEM((width - FRONT * TILE, heads * rank), bf16),
                pltpu.VMEM((width, heads * rank), bf16),
                pltpu.VMEM((heads, rank), bf16),
                pltpu.VMEM((1, count * seq), f32),
                pltpu.VMEM((2, LINES, width), bf16),
                pltpu.VMEM((1, lanes), f32),
                pltpu.VMEM((2 * chips, 1, lanes), f32),
                pltpu.SMEM(head_ratio.shape, i32),
                pltpu.SMEM(group_of.shape, i32),
                pltpu.SMEM(lengths.shape, i32),
                pltpu.VMEM((1, everyone), i32),
                pltpu.VMEM((count, seq), i32),
                pltpu.SemaphoreType.DMA((2 + pieces,)),
                pltpu.SemaphoreType.DMA,
                pltpu.SemaphoreType.REGULAR,
            ],
            compiler_params=pltpu.CompilerParams(
                collective_id=0, has_side_effects=True, vmem_limit_bytes=60 * 1024 * 1024
            ),
            name="advantages",
        )(rows, head_proj, *early, head_ratio, group_of, lengths, token_mask)

    return jax.shard_map(
        on_device,
        mesh=mesh,
        in_specs=(
            P(("dp", "head"), None, None),
            P("head", None, None),
            P("head", None),
            P(),
            P(),
            P(("dp", "head")),
            P(("dp", "head"), None),
        ),
        out_specs=P(("dp", "head"), None),
        check_vma=False,
    )
```

time: 13.9 us -> 13 us (0.935)
  Pallas kernels: 13.1 us -> 12.2 us
    pallas_call x1, Pallas kernels: 13.1 us -> 10.5 us  [on_device(): pl.pallas_call(functools.partial(kernel, chips), out_shape=pltpu.VMEM((co...]
    pallas_call x0 -> x1, Pallas kernels: none -> 1.66 us  [on_device(): pl.pallas_call(gather, out_shape=[pltpu.VMEM((FRONT * TILE, heads * rank)...]
where the time goes in v3:
time: 13 us; the launch traced here: 12.8 us
  Pallas kernels  12.2 us (94%)
  local copies, waits for them, and re-layouts  0.6 us (5%)
    pallas_call x1, Pallas kernels, on_device(): pl.pallas_call(functools.partial(kernel, chips), out_shape=pltpu.VMEM((co...  10.5 us
    pallas_call x1, Pallas kernels, on_device(): pl.pallas_call(gather, out_shape=[pltpu.VMEM((FRONT * TILE, heads * rank)...  1.66 us
    unnamed x1, local copies, waits for them, and re-layouts  0.6 us

profile of v3, /device:TPU:0, one launch (start us, length us, event | category | flops | bytes accessed | tf_op | source)
XLA Modules:
  0.0 12.8 jit_solution(841070079752173600)
XLA Ops:
  0.0 1.7 %gather.1 = (bf16[2048,256]{1,0:T(8,128)(2,1)S(1)}, bf16[8,3584]{1,0:T(8,128)(2,1)S(1)}, bf16[2,128]{1,0:T(2,128)(2,1)S(1)}, f32[1,256]{1,0:T(1,128)S(1)}) custom-call(bf16[128,8,3584]{2,1,0:T(8,128)(2,1)} %bitcast.2, bf16[2,3584,128]{2,1,0:T(8,128)(2,1)} %proj.3, bf16[2,128]{1,0:T(2,128)(2,1)} %readout.1, s32[4]{0:T(128)} %ratio.3, s32[2]{0:T(128)} %lens.3), custom_call_target="tpu_custom_call" | custom-call | tf_op jit(solution)/shard_map/gather/pallas_call | solution.py:413
  1.7 10.5 %advantages.1 = f32[2,512]{1,0:T(2,128)S(1)} custom-call(bf16[64,16,3584]{2,1,0:T(8,128)(2,1)} %bitcast.3, bf16[2,3584,128]{2,1,0:T(8,128)(2,1)} %proj.3, bf16[2048,256]{1,0:T(8,128)(2,1)S(1)} %get-tuple-element.9.w_front, bf16[8,3584]{1,0:T(8,128)(2,1)S(1)} %get-tuple-element.10.ends_own, bf16[2,128]{1,0:T(2,128)(2,1)S(1)} %get-tuple-element.11.out_own, ...), custom_call_target="tpu_custom_call" | custom-call | tf_op jit(solution)/shard_map/advantages/pallas_call | solution.py:432
  12.2 0.6 %copy.9 = f32[2,512]{1,0:T(2,128)} copy(f32[2,512]{1,0:T(2,128)S(1)} %advantages.1) | data formatting | bytes 8192

commit v4 on v3

--- a/solution.py
+++ b/solution.py
@@ -20,7 +20,7 @@
 TILE = 256
 UNITS = 2
 FAN = 32
-AHEAD = 4
+AHEAD = 2
 FRONT = 8
 
 
@@ -76,12 +76,15 @@
         sub = lax.broadcasted_iota(jnp.int32, (LINES, width), 0)
         picked = jnp.zeros((LINES, width), jnp.float32)
         for r in range(count):
-            at = sub == lax.rem(last[r], LINES)
-            row = jnp.sum(
-                jnp.where(at, found[r].astype(jnp.float32), 0.0), axis=0, keepdims=True
-            )
-            picked = jnp.where(sub == r, jnp.broadcast_to(row, (LINES, width)), picked)
-        ends_own[...] = picked.astype(jnp.bfloat16)
+            block = found[r].astype(jnp.float32)
+            turned = pltpu.roll(block, lax.rem(LINES + r - lax.rem(last[r], LINES), LINES), 0)
+            picked = jnp.where(sub == r, turned, picked)
+        lead = picked[:, :rank]
+        for k in range(heads):
+            at = sub[:, :rank] == count + k
+            lead = jnp.where(at, jnp.broadcast_to(wide[k : k + 1], (LINES, rank)), lead)
+        picked = jnp.concatenate([lead, picked[:, rank:]], axis=1)
+        ends_own[...] = picked[: count + heads].astype(jnp.bfloat16)
         with jax.named_scope("gather_w"):
             for copy in w_loads:
                 copy.wait()
@@ -97,7 +100,7 @@
 def kernel(
     chips,
     hidden, proj, w_front, ends_own, out_own, scale, ratio, groups, lens, mask, out,
-    rows_all, w_back, w_other, out_other, comb, ends, msg, slots,
+    rows_all, w_back, w_other, comb, ends, msg, slots,
     ratio_s, groups_s, lens_s, groups_v, mask_v,
     pair_recv, all_recv, here,
 ):
@@ -127,7 +130,7 @@
         lax.fori_loop(low, high, both, 0)
 
     def reader(values):
-        wide = values[...].astype(jnp.float32)
+        wide = values.astype(jnp.float32)
         line = lax.broadcasted_iota(jnp.int32, (PACK, rank), 0)
         parts = [
             jnp.where(line == k, jnp.broadcast_to(wide[k : k + 1], (PACK, rank)), 0.0)
@@ -156,19 +159,18 @@
             )
             for k in range(heads)
         ]
+
+        barrier = pltpu.get_barrier_semaphore()
+
+        def hello(place):
+            pl.semaphore_signal(barrier, inc=1, device_id=place, device_id_type=MESH)
+
+        hello((chip, 1 - core))
         for copy in w_loads:
             copy.start()
-
-        barrier = pltpu.get_barrier_semaphore()
-
-        def hello(place):
-            pl.semaphore_signal(barrier, inc=1, device_id=place, device_id_type=MESH)
-
-        hello((chip, 1 - core))
+        cores(hello, chip + 1, chips)
         for copy in h_loads + small:
             copy.start()
-        cores(hello, chip + 1, chips)
-        ends[0] = ends_own[...]
 
         def to_pair(src, dst, k):
             return pltpu.make_async_remote_copy(
@@ -176,13 +178,16 @@
                 device_id=(chip, 1 - core), device_id_type=MESH,
             )
 
-        send_ends = to_pair(ends_own, ends.at[1], 0)
-        send_out = to_pair(out_own, out_other, 1)
+        send_ends = to_pair(ends_own, ends, 0)
         def own_piece(span):
             return w_front if span[0] < FRONT else w_back
 
         send_w = [
-            to_pair(own_piece(span), w_other.at[columns(span)], 2 + d)
+            pltpu.make_async_remote_copy(
+                src_ref=own_piece(span), dst_ref=w_other.at[columns(span)],
+                send_sem=pair_send.at[1 + d], recv_sem=pair_recv.at[1 + d],
+                device_id=(chip, 1 - core), device_id_type=MESH,
+            )
             for d, span in enumerate(pieces)
         ]
 
@@ -236,12 +241,11 @@
                     add_tiles(own_tile, span)
             with jax.named_scope("own_scores"):
                 small[0].wait()
-                add_scores(out_own, mixture(ratio_s, core, heads), True)
+                add_scores(out_own[...], mixture(ratio_s, core, heads), True)
 
         with jax.named_scope("wait_barrier"):
             pl.semaphore_wait(barrier, 2 * chip + 1)
         send_ends.start()
-        send_out.start()
 
         @pl.when(ahead)
         def _():
@@ -260,8 +264,26 @@
             for unit, k in enumerate(turns[turn]):
                 pltpu.matmul_push_rhs(own_tile(k), turn % 2, unit)
 
-        for turn in range(2):
-            stage(turn)
+        lot = count + heads
+
+        def lines_of(k, own, other):
+            at = pl.ds(k * TILE, TILE)
+            blank = jnp.zeros((lot, TILE), jnp.float32)
+            stack = [
+                ends_own[:, at].astype(jnp.float32) if own else blank,
+                ends[:, at].astype(jnp.float32) if other else blank,
+                jnp.zeros((PACK - 2 * lot, TILE), jnp.float32),
+            ]
+            return jnp.concatenate(stack, axis=0).astype(jnp.bfloat16)
+
+        def add_lines(turn, own, other, load):
+            for unit, k in enumerate(turns[turn]):
+                pltpu.matmul_acc_lhs(brief[unit], lines_of(k, own, other), load)
+
+        stage(0)
+        stage(1)
+        add_lines(0, True, False, 0)
+        stage(2)
         with jax.named_scope("wait_w"):
             for copy in w_loads:
                 copy.wait()
@@ -273,24 +295,23 @@
         with jax.named_scope("wait_ends"):
             send_ends.wait_recv()
         with jax.named_scope("ends_dot"):
-            both = ends[...].reshape(2 * LINES, width)
-            for turn, units in enumerate(turns):
-                for unit, k in enumerate(units):
-                    at = k * TILE
-                    pltpu.matmul_acc_lhs(brief[unit], both[:, at : at + TILE], turn % 2)
+            add_lines(0, False, True, None)
+            for turn in range(1, len(turns)):
+                add_lines(turn, True, True, turn % 2)
                 if turn + 2 < len(turns):
                     stage(turn + 2)
             inner = pltpu.matmul_pop(brief[0]) + pltpu.matmul_pop(brief[1])
+            inner = inner[:LINES]
             active = jnp.tanh(inner).astype(jnp.bfloat16).astype(jnp.float32)
             part = jnp.sum(active * scale[...], axis=1, keepdims=True)
-            line = lax.broadcasted_iota(jnp.int32, (2 * LINES, lanes), 0)
-            lane = lax.broadcasted_iota(jnp.int32, (2 * LINES, lanes), 1)
+            line = lax.broadcasted_iota(jnp.int32, (LINES, lanes), 0)
+            lane = lax.broadcasted_iota(jnp.int32, (LINES, lanes), 1)
             mine = (line < count) & (lane == me * count + line)
-            theirs = (line >= LINES) & (line < LINES + count) & (
-                lane == (4 * chip + 1 - me) * count + line - LINES
+            theirs = (line >= lot) & (line < lot + count) & (
+                lane == (4 * chip + 1 - me) * count + line - lot
             )
             found = jnp.where(mine | theirs, part, 0.0)
-            found = found[:LINES] + found[LINES:]
+            found = found + pltpu.roll(found, lot, 0)
             note = sum([found[r : r + 1] for r in range(1, count)], found[:1])
             msg[...] = note
             slots[me] = note
@@ -323,19 +344,18 @@
                 copy.start()
             own_heads()
 
-        send_out.wait_recv()
         for d, span in enumerate(pieces):
             with jax.named_scope(f"wait_other{d}"):
                 send_w[d].wait_recv()
             with jax.named_scope(f"other{d}"):
                 add_tiles(other_tile, span)
         with jax.named_scope("other_scores"):
-            add_scores(out_other, mixture(ratio_s, 1 - core, heads), False)
+            values = ends[:, :rank].astype(jnp.float32)[count:]
+            add_scores(values, mixture(ratio_s, 1 - core, heads), False)
 
         for copy in small[1:]:
             copy.wait()
         send_ends.wait_send()
-        send_out.wait_send()
         for copy in send_w:
             copy.wait_send()
         rest = slots.at[pl.ds(0, devices - 1)]
@@ -348,11 +368,11 @@
         body,
         [[acc(unit, TILE) for _ in range(blocks)] for unit in range(UNITS)],
         [[acc(unit, PACK) for _ in range(blocks)] for unit in range(UNITS)],
-        [acc(unit, 2 * LINES) for unit in range(UNITS)],
+        [acc(unit, PACK) for unit in range(UNITS)],
         pltpu.SemaphoreType.DMA((2,)),
         pltpu.SemaphoreType.DMA((heads,)),
         pltpu.SemaphoreType.DMA((5,)),
-        pltpu.SemaphoreType.DMA((2 + len(pieces),)),
+        pltpu.SemaphoreType.DMA((1 + len(pieces),)),
         pltpu.SemaphoreType.DMA((1,)),
     )
 
@@ -414,7 +434,7 @@
             gather,
             out_shape=[
                 pltpu.VMEM((FRONT * TILE, heads * rank), bf16),
-                pltpu.VMEM((LINES, width), bf16),
+                pltpu.VMEM((count + heads, width), bf16),
                 pltpu.VMEM((heads, rank), bf16),
                 pltpu.VMEM((1, heads * rank), f32),
             ],
@@ -438,9 +458,8 @@
                 pltpu.VMEM((count * seq // PACK, PACK, width), bf16),
                 pltpu.VMEM((width - FRONT * TILE, heads * rank), bf16),
                 pltpu.VMEM((width, heads * rank), bf16),
-                pltpu.VMEM((heads, rank), bf16),
                 pltpu.VMEM((1, count * seq), f32),
-                pltpu.VMEM((2, LINES, width), bf16),
+                pltpu.VMEM((count + heads, width), bf16),
                 pltpu.VMEM((1, lanes), f32),
                 pltpu.VMEM((2 * chips, 1, lanes), f32),
                 pltpu.SMEM(head_ratio.shape, i32),
@@ -448,7 +467,7 @@
                 pltpu.SMEM(lengths.shape, i32),
                 pltpu.VMEM((1, everyone), i32),
                 pltpu.VMEM((count, seq), i32),
-                pltpu.SemaphoreType.DMA((2 + pieces,)),
+                pltpu.SemaphoreType.DMA((1 + pieces,)),
                 pltpu.SemaphoreType.DMA,
                 pltpu.SemaphoreType.REGULAR,
             ],

time: 13 us -> 12.8 us (0.985)
  no operation moved by 1% of the time
where the time goes in v4:
time: 12.8 us; the launch traced here: 12.7 us
  Pallas kernels  12.1 us (95%)
  local copies, waits for them, and re-layouts  0.6 us (5%)
    pallas_call x1, Pallas kernels, on_device(): pl.pallas_call(functools.partial(kernel, chips), out_shape=pltpu.VMEM((co...  10.5 us
    pallas_call x1, Pallas kernels, on_device(): pl.pallas_call(gather, out_shape=[pltpu.VMEM((FRONT * TILE, heads * rank)...  1.62 us
    unnamed x1, local copies, waits for them, and re-layouts  0.6 us

profile of v4, /device:TPU:0, one launch (start us, length us, event | category | flops | bytes accessed | tf_op | source)
XLA Modules:
  0.0 12.7 jit_solution(5762667580642218763)
XLA Ops:
  0.0 1.6 %gather.1 = (bf16[2048,256]{1,0:T(8,128)(2,1)S(1)}, bf16[4,3584]{1,0:T(4,128)(2,1)S(1)}, bf16[2,128]{1,0:T(2,128)(2,1)S(1)}, f32[1,256]{1,0:T(1,128)S(1)}) custom-call(bf16[128,8,3584]{2,1,0:T(8,128)(2,1)} %bitcast.2, bf16[2,3584,128]{2,1,0:T(8,128)(2,1)} %proj.3, bf16[2,128]{1,0:T(2,128)(2,1)} %readout.1, s32[4]{0:T(128)} %ratio.3, s32[2]{0:T(128)} %lens.3), custom_call_target="tpu_custom_call" | custom-call | tf_op jit(solution)/shard_map/gather/pallas_call | solution.py:433
  1.6 10.5 %advantages.1 = f32[2,512]{1,0:T(2,128)S(1)} custom-call(bf16[64,16,3584]{2,1,0:T(8,128)(2,1)} %bitcast.3, bf16[2,3584,128]{2,1,0:T(8,128)(2,1)} %proj.3, bf16[2048,256]{1,0:T(8,128)(2,1)S(1)} %get-tuple-element.9.w_front, bf16[4,3584]{1,0:T(4,128)(2,1)S(1)} %get-tuple-element.10.ends_own, bf16[2,128]{1,0:T(2,128)(2,1)S(1)} %get-tuple-element.11.out_own, ...), custom_call_target="tpu_custom_call" | custom-call | tf_op jit(solution)/shard_map/advantages/pallas_call | solution.py:452
  12.1 0.6 %copy.9 = f32[2,512]{1,0:T(2,128)} copy(f32[2,512]{1,0:T(2,128)S(1)} %advantages.1) | data formatting | bytes 8192

commit v5 on v4

--- a/solution.py
+++ b/solution.py
@@ -19,8 +19,9 @@
 LINES = 8
 TILE = 256
 UNITS = 2
-FAN = 32
 AHEAD = 2
+LEAD = 16
+WAVES = 2
 FRONT = 8
 
 
@@ -111,12 +112,15 @@
     devices = 2 * chips
     me = 2 * chip + core
     total_rows = count * seq
-    lanes = msg.shape[1]
+    everyone = groups.shape[0]
+    slot = core * chips + chip
+    wave = chips // WAVES
     tiles = width // TILE
     spans = [range(FRONT), range(FRONT, tiles)]
     blocks = total_rows // UNITS // TILE
     pieces = [range(FRONT), range(FRONT, tiles)]
     ahead = chip < max(1, chips // AHEAD)
+    lead = chip < max(1, chips // LEAD)
 
     def columns(span):
         return pl.ds(span[0] * TILE, len(span) * TILE)
@@ -243,6 +247,16 @@
                 small[0].wait()
                 add_scores(out_own[...], mixture(ratio_s, core, heads), True)
 
+        def other_heads():
+            for d, span in enumerate(pieces):
+                with jax.named_scope(f"wait_other{d}"):
+                    send_w[d].wait_recv()
+                with jax.named_scope(f"other{d}"):
+                    add_tiles(other_tile, span)
+            with jax.named_scope("other_scores"):
+                values = ends[:, :rank].astype(jnp.float32)[count:]
+                add_scores(values, mixture(ratio_s, 1 - core, heads), False)
+
         with jax.named_scope("wait_barrier"):
             pl.semaphore_wait(barrier, 2 * chip + 1)
         send_ends.start()
@@ -253,7 +267,7 @@
 
         cores(
             lambda place: pl.semaphore_signal(
-                here, inc=1, device_id=place, device_id_type=MESH
+                here.at[lax.div(chip, wave)], inc=1, device_id=place, device_id_type=MESH
             ),
             0, chip,
         )
@@ -303,22 +317,20 @@
             inner = pltpu.matmul_pop(brief[0]) + pltpu.matmul_pop(brief[1])
             inner = inner[:LINES]
             active = jnp.tanh(inner).astype(jnp.bfloat16).astype(jnp.float32)
-            part = jnp.sum(active * scale[...], axis=1, keepdims=True)
-            line = lax.broadcasted_iota(jnp.int32, (LINES, lanes), 0)
-            lane = lax.broadcasted_iota(jnp.int32, (LINES, lanes), 1)
-            mine = (line < count) & (lane == me * count + line)
-            theirs = (line >= lot) & (line < lot + count) & (
-                lane == (4 * chip + 1 - me) * count + line - lot
-            )
-            found = jnp.where(mine | theirs, part, 0.0)
-            found = found + pltpu.roll(found, lot, 0)
-            note = sum([found[r : r + 1] for r in range(1, count)], found[:1])
+            wide = active * scale[...]
+            part = sum(
+                [wide[:, k * rank : (k + 1) * rank] for k in range(1, heads)], wide[:, :rank]
+            )
+            line = lax.broadcasted_iota(jnp.int32, (LINES, rank), 0)
+            own = pltpu.roll(part, core * count, 0)
+            other = pltpu.roll(part, LINES - lot + (1 - core) * count, 0)
+            note = jnp.where(lax.div(line, count) == core, own, other)[: 2 * count]
             msg[...] = note
-            slots[me] = note
+            slots[slot] = note
 
         def tell(place):
             pltpu.make_async_remote_copy(
-                src_ref=msg, dst_ref=slots.at[me], send_sem=all_send.at[0],
+                src_ref=msg, dst_ref=slots.at[slot], send_sem=all_send.at[0],
                 recv_sem=all_recv, device_id=place, device_id_type=MESH,
             ).start()
 
@@ -330,13 +342,25 @@
         def _():
             own_heads()
 
-        @pl.when(chip < chips - 1)
+        def send_higher(k):
+            low, high = jnp.maximum(k * wave, chip + 1), (k + 1) * wave
+
+            @pl.when(low < high)
+            def _():
+                with jax.named_scope(f"wait_higher{k}"):
+                    pl.semaphore_wait(here.at[k], 2 * (high - low))
+                with jax.named_scope(f"send_higher{k}"):
+                    cores(tell, low, high)
+
+        for k in range(WAVES // 2):
+            send_higher(k)
+
+        @pl.when(lead)
         def _():
-            with jax.named_scope("wait_higher"):
-                pl.semaphore_wait(here, devices - 2 - 2 * chip)
-
-        with jax.named_scope("send_higher"):
-            cores(tell, chip + 1, chips)
+            other_heads()
+
+        for k in range(WAVES // 2, WAVES):
+            send_higher(k)
 
         @pl.when(jnp.logical_not(ahead))
         def _():
@@ -344,14 +368,9 @@
                 copy.start()
             own_heads()
 
-        for d, span in enumerate(pieces):
-            with jax.named_scope(f"wait_other{d}"):
-                send_w[d].wait_recv()
-            with jax.named_scope(f"other{d}"):
-                add_tiles(other_tile, span)
-        with jax.named_scope("other_scores"):
-            values = ends[:, :rank].astype(jnp.float32)[count:]
-            add_scores(values, mixture(ratio_s, 1 - core, heads), False)
+        @pl.when(jnp.logical_not(lead))
+        def _():
+            other_heads()
 
         for copy in small[1:]:
             copy.wait()
@@ -376,17 +395,17 @@
         pltpu.SemaphoreType.DMA((1,)),
     )
 
-    labels = groups_v[...]
-    shape = (count, labels.shape[1])
-    rollout = lax.broadcasted_iota(jnp.int32, shape, 0)
-    lane_of = lax.broadcasted_iota(jnp.int32, shape, 1)
-    group = jnp.zeros(shape, jnp.int32)
+    across = lax.broadcasted_iota(jnp.int32, (everyone, everyone), 1)
+    down = lax.broadcasted_iota(jnp.int32, (everyone, everyone), 0)
+    labels = jnp.broadcast_to(groups_v[...].astype(jnp.float32), (everyone, everyone))
+    labels = jnp.sum(jnp.where(across == down, labels, 0.0), axis=1, keepdims=True)
+    rollout = lax.broadcasted_iota(jnp.int32, (everyone, 1), 0)
+    members = [labels == groups_s[me * count + r].astype(jnp.float32) for r in range(count)]
+    owners = [rollout == me * count + r for r in range(count)]
     length = jnp.zeros((count, seq), jnp.int32)
     line = lax.broadcasted_iota(jnp.int32, (count, seq), 0)
     for r in range(count):
-        group = jnp.where(rollout == r, groups_s[me * count + r], group)
         length = jnp.where(line == r, lens_s[r], length)
-    member = jnp.broadcast_to(labels, shape) == group
     place = lax.broadcasted_iota(jnp.int32, (count, seq), 1)
     valid = (place < length) & (mask_v[...] == 1)
     tokens = token_weight * jnp.concatenate(
@@ -398,21 +417,19 @@
         pltpu.make_async_copy(rest, rest, all_recv).wait()
 
     with jax.named_scope("final"):
-        level = [slots[k] for k in range(min(devices, FAN))]
-        for k in range(FAN, devices):
-            level[k % FAN] = level[k % FAN] + slots[k]
-        while len(level) > 1:
-            level = [sum(level[k + 1 : k + 2], level[k]) for k in range(0, len(level), 2)]
-        reward = level[0][:, : labels.shape[1]]
-        wide = jnp.broadcast_to(reward, shape)
-        own = jnp.sum(
-            jnp.where(lane_of == me * count + rollout, wide, 0.0), axis=1, keepdims=True
-        )
-        mean = jnp.sum(jnp.where(member, wide, 0.0), axis=1, keepdims=True) * (1 / GROUP)
-        gap = wide - mean
-        var = jnp.sum(jnp.where(member, gap * gap, 0.0), axis=1, keepdims=True) * (1 / GROUP)
-        best = jnp.max(jnp.where(member, wide, -jnp.inf), axis=1, keepdims=True)
-        base = (own - mean) * lax.rsqrt(var + var_offset) - gap_weight * (best - own)
+        total = slots[pl.ds(0, chips)] + slots[pl.ds(chips, chips)]
+        reward = jnp.sum(total.reshape(everyone, rank), axis=1, keepdims=True)
+        base = jnp.zeros((count, seq), jnp.float32)
+        for r in range(count):
+            own = jnp.sum(jnp.where(owners[r], reward, 0.0), axis=0, keepdims=True)
+            mean = jnp.sum(jnp.where(members[r], reward, 0.0), axis=0, keepdims=True)
+            mean = mean * (1 / GROUP)
+            gap = reward - mean
+            var = jnp.sum(jnp.where(members[r], gap * gap, 0.0), axis=0, keepdims=True)
+            var = var * (1 / GROUP)
+            best = jnp.max(jnp.where(members[r], reward, -jnp.inf), axis=0, keepdims=True)
+            one = (own - mean) * lax.rsqrt(var + var_offset) - gap_weight * (best - own)
+            base = jnp.where(line == r, jnp.broadcast_to(one, (count, seq)), base)
         shaped = base + tokens
         out[...] = jnp.where(valid, jnp.clip(shaped, -clip_limit, clip_limit), 0.0)
 
@@ -424,7 +441,6 @@
         count, seq, width = hidden.shape
         heads, _, rank = head_proj.shape
         everyone = group_of.shape[0]
-        lanes = -(-everyone // 128) * 128
         pieces = 2
         hbm = pl.BlockSpec(memory_space=pltpu.HBM)
         bf16, f32, i32 = jnp.bfloat16, jnp.float32, jnp.int32
@@ -460,8 +476,8 @@
                 pltpu.VMEM((width, heads * rank), bf16),
                 pltpu.VMEM((1, count * seq), f32),
                 pltpu.VMEM((count + heads, width), bf16),
-                pltpu.VMEM((1, lanes), f32),
-                pltpu.VMEM((2 * chips, 1, lanes), f32),
+                pltpu.VMEM((2 * count, rank), f32),
+                pltpu.VMEM((2 * chips, 2 * count, rank), f32),
                 pltpu.SMEM(head_ratio.shape, i32),
                 pltpu.SMEM(group_of.shape, i32),
                 pltpu.SMEM(lengths.shape, i32),
@@ -469,7 +485,7 @@
                 pltpu.VMEM((count, seq), i32),
                 pltpu.SemaphoreType.DMA((1 + pieces,)),
                 pltpu.SemaphoreType.DMA,
-                pltpu.SemaphoreType.REGULAR,
+                pltpu.SemaphoreType.REGULAR((WAVES,)),
             ],
             compiler_params=pltpu.CompilerParams(
                 collective_id=0, has_side_effects=True, vmem_limit_bytes=60 * 1024 * 1024

time: 12.8 us -> 12.8 us (level)
  no operation moved by 1% of the time
where the time goes in v5:
time: 12.8 us; the launch traced here: 12.6 us
  Pallas kernels  12 us (94%)
  local copies, waits for them, and re-layouts  0.6 us (5%)
    pallas_call x1, Pallas kernels, on_device(): pl.pallas_call(functools.partial(kernel, chips), out_shape=pltpu.VMEM((co...  10.4 us
    pallas_call x1, Pallas kernels, on_device(): pl.pallas_call(gather, out_shape=[pltpu.VMEM((FRONT * TILE, heads * rank)...  1.62 us
    unnamed x1, local copies, waits for them, and re-layouts  0.6 us

profile of v5, /device:TPU:0, one launch (start us, length us, event | category | flops | bytes accessed | tf_op | source)
XLA Modules:
  0.0 12.6 jit_solution(14223464105316929691)
XLA Ops:
  0.0 1.6 %gather.1 = (bf16[2048,256]{1,0:T(8,128)(2,1)S(1)}, bf16[4,3584]{1,0:T(4,128)(2,1)S(1)}, bf16[2,128]{1,0:T(2,128)(2,1)S(1)}, f32[1,256]{1,0:T(1,128)S(1)}) custom-call(bf16[128,8,3584]{2,1,0:T(8,128)(2,1)} %bitcast.2, bf16[2,3584,128]{2,1,0:T(8,128)(2,1)} %proj.3, bf16[2,128]{1,0:T(2,128)(2,1)} %readout.1, s32[4]{0:T(128)} %ratio.3, s32[2]{0:T(128)} %lens.3), custom_call_target="tpu_custom_call" | custom-call | tf_op jit(solution)/shard_map/gather/pallas_call | solution.py:449
  1.6 10.4 %advantages.1 = f32[2,512]{1,0:T(2,128)S(1)} custom-call(bf16[64,16,3584]{2,1,0:T(8,128)(2,1)} %bitcast.3, bf16[2,3584,128]{2,1,0:T(8,128)(2,1)} %proj.3, bf16[2048,256]{1,0:T(8,128)(2,1)S(1)} %get-tuple-element.9.w_front, bf16[4,3584]{1,0:T(4,128)(2,1)S(1)} %get-tuple-element.10.ends_own, bf16[2,128]{1,0:T(2,128)(2,1)S(1)} %get-tuple-element.11.out_own, ...), custom_call_target="tpu_custom_call" | custom-call | tf_op jit(solution)/shard_map/advantages/pallas_call | solution.py:468
  12.0 0.6 %copy.9 = f32[2,512]{1,0:T(2,128)} copy(f32[2,512]{1,0:T(2,128)S(1)} %advantages.1) | data formatting | bytes 8192

commit v6 on v5

--- a/solution.py
+++ b/solution.py
@@ -22,7 +22,7 @@
 AHEAD = 2
 LEAD = 16
 WAVES = 2
-FRONT = 8
+FRONT = 9
 
 
 def mixture(ratio_s, part, heads):
@@ -335,7 +335,12 @@
             ).start()
 
         with jax.named_scope("send_lower"):
-            cores(tell, 0, chip)
+            @pl.when(chip > 0)
+            def _():
+                tell((0, core))
+                tell((0, 1 - core))
+
+            cores(tell, 1, chip)
             tell((chip, 1 - core))
 
         @pl.when(ahead)

time: 12.8 us -> 12.8 us (level)
  no operation moved by 1% of the time
where the time goes in v6:
time: 12.8 us; the launch traced here: 12.6 us
  Pallas kernels  12 us (94%)
  local copies, waits for them, and re-layouts  0.6 us (5%)
    pallas_call x1, Pallas kernels, on_device(): pl.pallas_call(functools.partial(kernel, chips), out_shape=pltpu.VMEM((co...  10.4 us
    pallas_call x1, Pallas kernels, on_device(): pl.pallas_call(gather, out_shape=[pltpu.VMEM((FRONT * TILE, heads * rank)...  1.63 us
    unnamed x1, local copies, waits for them, and re-layouts  0.6 us

profile of v6, /device:TPU:0, one launch (start us, length us, event | category | flops | bytes accessed | tf_op | source)
XLA Modules:
  0.0 12.6 jit_solution(17745693479098389174)
XLA Ops:
  0.0 1.6 %gather.1 = (bf16[2304,256]{1,0:T(8,128)(2,1)S(1)}, bf16[4,3584]{1,0:T(4,128)(2,1)S(1)}, bf16[2,128]{1,0:T(2,128)(2,1)S(1)}, f32[1,256]{1,0:T(1,128)S(1)}) custom-call(bf16[128,8,3584]{2,1,0:T(8,128)(2,1)} %bitcast.2, bf16[2,3584,128]{2,1,0:T(8,128)(2,1)} %proj.3, bf16[2,128]{1,0:T(2,128)(2,1)} %readout.1, s32[4]{0:T(128)} %ratio.3, s32[2]{0:T(128)} %lens.3), custom_call_target="tpu_custom_call" | custom-call | tf_op jit(solution)/shard_map/gather/pallas_call | solution.py:454
  1.6 10.4 %advantages.1 = f32[2,512]{1,0:T(2,128)S(1)} custom-call(bf16[64,16,3584]{2,1,0:T(8,128)(2,1)} %bitcast.3, bf16[2,3584,128]{2,1,0:T(8,128)(2,1)} %proj.3, bf16[2304,256]{1,0:T(8,128)(2,1)S(1)} %get-tuple-element.9.w_front, bf16[4,3584]{1,0:T(4,128)(2,1)S(1)} %get-tuple-element.10.ends_own, bf16[2,128]{1,0:T(2,128)(2,1)S(1)} %get-tuple-element.11.out_own, ...), custom_call_target="tpu_custom_call" | custom-call | tf_op jit(solution)/shard_map/advantages/pallas_call | solution.py:473
  12.0 0.6 %copy.9 = f32[2,512]{1,0:T(2,128)} copy(f32[2,512]{1,0:T(2,128)S(1)} %advantages.1) | data formatting | bytes 8192
